TPU v7x, 32 devices: a whole 2x2x4 slice. The times are simulated.
32 devices in a mesh: expert: 16 (over z, x, core), tensor: 2 (over y).
Axes of the slice: x: 2, y: 2, z: 4, core: 2. Of those that a mesh axis runs over, the one named last changes fastest.
Arguments:
- tokens: bfloat16 [1024, 2048], P('expert'), may hold values from -6 to 6
- expert_ids: int32 [1024, 6], replicated, may hold values from 0 to 31, all different within a row; in each aligned block of 1024 rows (0 to 1023, 1024 to 2047, ...) at most 256 rows name the same one
- gate_probs: float32 [1024, 6], replicated, may hold values from 0.02 to 0.6
- w_gate: bfloat16 [32, 2048, 1408], P('expert', None, 'tensor'), may hold values from -0.125 to 0.125
- w_up: bfloat16 [32, 2048, 1408], P('expert', None, 'tensor'), may hold values from -0.125 to 0.125
- w_down: bfloat16 [32, 1408, 2048], P('expert', 'tensor'), may hold values from -0.15625 to 0.15625
- shared_gate: bfloat16 [2048, 2816], P(None, 'tensor'), may hold values from -0.125 to 0.125
- shared_up: bfloat16 [2048, 2816], P(None, 'tensor'), may hold values from -0.125 to 0.125
- shared_down: bfloat16 [2816, 2048], P('tensor'), may hold values from -0.109375 to 0.109375
Outputs:
- layer_out: bfloat16 [1024, 2048], P('expert')
Inputs may be any that keep to these rules, and one draw needn't show every extreme that they name: `expert_ids`: each row names 6 different experts. Over all 1024 tokens no expert is named more than 256 times, a bound that some block reaches.
All inputs are finite; a program needn't handle non-finite values.
Results may differ from a plain program's by a relative error of at most 0.011.
Values may be sent and summed in bfloat16 or wider, within the bound.
A program may use at most 64 MiB of HBM per device.

v0:
```python
import math

import jax
import jax.numpy as jnp
from jax import lax
from jax.sharding import PartitionSpec as P


def place_rows(expert_ids, gate_probs, expert):
    hits = expert_ids == expert
    row_hit = jnp.sum(hits.astype(jnp.float32), axis=1)
    total_rows = row_hit.shape[0]
    block = math.gcd(total_rows, 128)
    blocks = row_hit.reshape(total_rows // block, block)
    lower = jnp.arange(block, dtype=jnp.int32)
    strict = (lower[:, None] < lower[None, :]).astype(jnp.float32)
    inside = jnp.dot(blocks, strict, precision=lax.Precision.HIGHEST)
    sums = jnp.sum(blocks, axis=1)
    offsets = jnp.cumsum(sums) - sums
    before = (inside + offsets[:, None]).reshape(total_rows)
    target = jnp.where(row_hit > 0.5, before, -1.0).astype(jnp.int32)
    weight = jnp.sum(jnp.where(hits, gate_probs, 0.0), axis=1)
    return (target, weight)


def body(tokens, expert_ids, gate_probs, w_gate, w_up, w_down, shared_gate, shared_up, shared_down):
    local_count = w_gate.shape[0]
    own_rows = tokens.shape[0]
    capacity = 4 * own_rows
    first_expert = lax.axis_index("expert") * local_count
    local_experts = first_expert + jnp.arange(local_count, dtype=jnp.int32)
    targets, weights = jax.vmap(lambda expert: place_rows(expert_ids, gate_probs, expert))(
        local_experts
    )
    positions = jnp.arange(capacity, dtype=jnp.int32)
    columns = targets
    picker = (positions[None, :, None] == columns[:, None, :]).astype(jnp.bfloat16)
    collected = jnp.einsum(
        "lcr,rd->lcd",
        picker,
        lax.all_gather(tokens, "expert", axis=0, tiled=True),
        preferred_element_type=jnp.float32,
    )
    dispatched = collected.astype(jnp.bfloat16)
    gate = jnp.einsum("lcd,ldf->lcf", dispatched, w_gate, preferred_element_type=jnp.float32)
    upper = jnp.einsum("lcd,ldf->lcf", dispatched, w_up, preferred_element_type=jnp.float32)
    hidden = (jax.nn.silu(gate) * upper).astype(jnp.bfloat16)
    partial_value = jnp.einsum("lcf,lfd->lcd", hidden, w_down, preferred_element_type=jnp.float32)
    sgate = jnp.dot(tokens, shared_gate, preferred_element_type=jnp.float32)
    supper = jnp.dot(tokens, shared_up, preferred_element_type=jnp.float32)
    shared_hidden = (jax.nn.silu(sgate) * supper).astype(jnp.bfloat16)
    shared_part = jnp.dot(shared_hidden, shared_down, preferred_element_type=jnp.float32)
    width_sum = lax.psum_scatter(
        partial_value.astype(jnp.bfloat16), "tensor", scatter_dimension=2, tiled=True
    ).astype(jnp.float32)
    high_part = width_sum.astype(jnp.bfloat16)
    low_part = (width_sum - high_part.astype(jnp.float32)).astype(jnp.bfloat16)
    columns = targets
    picker = (columns[:, :, None] == positions[None, None, :]).astype(jnp.bfloat16)
    picked = jnp.einsum("lrc,lcd->lrd", picker, high_part, preferred_element_type=jnp.float32)
    picked = picked + jnp.einsum(
        "lrc,lcd->lrd", picker, low_part, preferred_element_type=jnp.float32
    )
    factor = jnp.where(columns >= 0, weights, 0.0)
    routed = lax.psum_scatter(
        jnp.sum(factor[:, :, None] * picked, axis=0).astype(jnp.bfloat16),
        "expert",
        scatter_dimension=0,
        tiled=True,
    ).astype(jnp.float32)
    shared = lax.psum_scatter(shared_part, "tensor", scatter_dimension=1, tiled=True)
    mixed = (shared + routed).astype(jnp.bfloat16)
    return lax.all_gather(mixed, "tensor", axis=1, tiled=True)


def solution(mesh):
    placed = (
        P("expert", None),
        P(),
        P(),
        P("expert", None, "tensor"),
        P("expert", None, "tensor"),
        P("expert", "tensor", None),
        P(None, "tensor"),
        P(None, "tensor"),
        P("tensor", None),
    )
    return jax.shard_map(
        body, mesh=mesh, in_specs=placed, out_specs=P("expert", None), check_vma=False
    )
```

profile of v0, /device:TPU:0, one launch (start us, length us, event | category | flops | bytes accessed | tf_op | source)
XLA Modules:
  0.0 209.0 jit_solution(4812422969887766233)
XLA Ops:
  6.5 0.0 all-gather.2.cloned.1.call-start
  6.5 0.7 all-gather.2.cloned.1.call-update
  7.3 0.0 reduce-scatter.6.cloned.1.call-start
  7.3 0.9 fusion.22
  8.2 0.1 bitcast_reduce_fusion
  8.3 0.2 reduce_window_sum.11
  8.5 0.1 fusion.8
  8.6 0.1 compare_select_fusion.1
  8.7 53.9 %all-gather.2.cloned.1.call-done = bf16[1024,2048]{1,0:T(8,128)(2,1)} async-done(((bf16[64,2048]{1,0:T(8,128)(2,1)}), bf16[1024,2048]{1,0:T(8,128)(2,1)}) %all-gather.2.cloned.1.call-update) | async-done | bytes 4194320 | tf_op jit(solution)/shard_map/all_gather | solution.py:41
  62.6 4.5 %fusion.2 = bf16[2,256,2048]{2,1,0:T(8,128)(2,1)S(1)} fusion(bf16[1024,2048]{1,0:T(8,128)(2,1)} %all-gather.2.cloned.1.call-done, s32[2,1024]{1,0:T(2,128)S(1)} %get-tuple-element.8), kind=kOutput, calls=%fused_computation.3 | convolution fusion | flops 2149056512 | bytes 6299648 | tf_op jit(solution)/shard_map/lcr,rd->lcd/dot_general | solution.py:38
  67.1 5.4 %fusion.30 = f32[2,256,704]{1,2,0:T(8,128)} fusion(bf16[2,256,2048]{2,1,0:T(8,128)(2,1)S(1)} %fusion.2, bf16[2,2048,704]{1,2,0:T(8,128)(2,1)} %param.12), kind=kOutput, calls=%fused_computation.42 | convolution fusion | flops 1476395008 | bytes 9306112 | tf_op jit(solution)/shard_map/lcd,ldf->lcf/dot_general | solution.py:45
  72.6 0.0 copy-start.1
  72.6 9.6 %convolution_convert_fusion = bf16[2,256,2048]{2,1,0:T(8,128)(2,1)} fusion(bf16[2,704,2048]{2,1,0:T(8,128)(2,1)} %param.14, bf16[2,256,2048]{2,1,0:T(8,128)(2,1)S(1)} %fusion.2, bf16[2,2048,704]{1,2,0:T(8,128)(2,1)} %param.13, f32[2,256,704]{1,2,0:T(8,128)} %fusion.30), kind=kOutput, calls=%fused_computation.4 | convolution fusion | flops 2956001280 | bytes 17170432 | tf_op jit(solution)/shard_map/lcf,lfd->lcd/dot_general | solution.py:48
  82.2 0.0 reduce-scatter.6.cloned.1.call-update
  82.2 0.0 reduce-scatter.4.cloned.1.call-start
  82.2 0.0 copy-done.1
  82.2 3.7 %fusion.29 = f32[64,1408]{1,0:T(8,128)S(1)} fusion(bf16[64,2048]{1,0:T(8,128)(2,1)S(1)} %copy-done.1, bf16[2048,1408]{1,0:T(8,128)(2,1)} %param.15), kind=kOutput, calls=%fused_computation.41 | convolution fusion | flops 369098752 | bytes 6389760 | tf_op jit(solution)/shard_map/dot_general | solution.py:49
  85.9 7.8 %fusion.9 = f32[64,2048]{1,0:T(8,128)} fusion(bf16[1408,2048]{1,0:T(8,128)(2,1)} %param.17, bf16[64,2048]{1,0:T(8,128)(2,1)S(1)} %copy-done.1, bf16[2048,1408]{1,0:T(8,128)(2,1)} %param.16, f32[64,1408]{1,0:T(8,128)S(1)} %fusion.29), kind=kOutput, calls=%fused_computation.15 | convolution fusion | flops 738738176 | bytes 12681216 | tf_op jit(solution)/shard_map/dot_general | solution.py:52
  93.8 0.0 reduce-scatter.4.cloned.1.call-update
  93.8 0.0 reduce-scatter.8.cloned.1.call-start
  93.9 18.9 %reduce-scatter.6.cloned.1.call-done = bf16[2,256,1024]{2,1,0:T(8,128)(2,1)} async-done(((bf16[2,256,2048]{2,1,0:T(8,128)(2,1)}), bf16[2,256,1024]{2,1,0:T(8,128)(2,1)}) %reduce-scatter.6.cloned.1.call-update) | async-done | bytes 1048592 | tf_op jit(solution)/shard_map/reduce_scatter | solution.py:53
  112.8 0.0 copy-start
  112.8 2.7 %fusion.6 = f32[2,1024,1024]{2,1,0:T(8,128)S(1)} fusion(bf16[2,256,1024]{2,1,0:T(8,128)(2,1)} %reduce-scatter.6.cloned.1.call-done, s32[2,1024]{1,0:T(2,128)S(1)} %get-tuple-element.8), kind=kOutput, calls=%fused_computation.10 | convolution fusion | flops 1074266112 | bytes 9445376 | tf_op jit(solution)/shard_map/lrc,lcd->lrd/dot_general | solution.py:60
  115.5 0.0 copy-done
  115.5 3.8 %multiply_reduce_fusion = bf16[1024,1024]{1,0:T(8,128)(2,1)} fusion(f32[2,1024,1024]{2,1,0:T(8,128)S(1)} %fusion.6, f32[2,1024]{1,0:T(2,128)S(1)} %get-tuple-element.7, bf16[2,256,1024]{2,1,0:T(8,128)(2,1)S(1)} %copy-done, s32[2,1024]{1,0:T(2,128)S(1)} %get-tuple-element.8), kind=kOutput, calls=%fused_computation | convolution fusion | flops 1081081856 | bytes 11550720 | tf_op jit(solution)/shard_map/lrc,lcd->lrd/dot_general | solution.py:61
  119.3 0.0 reduce-scatter.8.cloned.1.call-update
  119.3 10.3 %reduce-scatter.4.cloned.1.call-done = f32[64,1024]{1,0:T(8,128)} async-done(((f32[64,2048]{1,0:T(8,128)}), f32[64,1024]{1,0:T(8,128)}) %reduce-scatter.4.cloned.1.call-update) | async-done | bytes 262160 | tf_op jit(solution)/shard_map/reduce_scatter | solution.py:71
  129.7 65.4 %reduce-scatter.8.cloned.1.call-done = bf16[64,1024]{1,0:T(8,128)(2,1)} async-done(((bf16[1024,1024]{1,0:T(8,128)(2,1)}), bf16[64,1024]{1,0:T(8,128)(2,1)}) %reduce-scatter.8.cloned.1.call-update) | async-done | bytes 131088 | tf_op jit(solution)/shard_map/reduce_scatter | solution.py:65
  195.1 1.0 add_convert_fusion
  196.1 5.6 %all_gather.7 = bf16[64,2048]{1,0:T(8,128)(2,1)S(1)} all-gather(bf16[64,1024]{1,0:T(8,128)(2,1)S(1)} %add_convert_fusion), channel_id=1, replica_groups=mesh['expert'=16,'tensor'=2] {'tensor'}, dimensions={1}, use_global_device_ids=true | all-gather | bytes 393216 | tf_op jit(solution)/shard_map/all_gather | solution.py:73
  201.7 0.7 copy.22
  (2 shorter events, 0.0 us)
Async XLA Ops:
  6.5 56.1 %all-gather.2.cloned.1.call-start = ((), (), s32[]{:S(2)}) async-start(), calls=%async_computation.4 | async-start | bytes 4456448 | tf_op jit(solution)/shard_map/all_gather | solution.py:41
  7.3 105.5 %reduce-scatter.6.cloned.1.call-start = ((), (), s32[]{:S(2)}) async-start(), calls=%async_computation.5 | async-start | bytes 3145728 | tf_op jit(solution)/shard_map/reduce_scatter | solution.py:53
  72.6 9.7 %copy-start.1 = (bf16[64,2048]{1,0:T(8,128)(2,1)S(1)}, bf16[64,2048]{1,0:T(8,128)(2,1)}, u32[]{:S(2)}) copy-start(bf16[64,2048]{1,0:T(8,128)(2,1)} %param.9) | copy-start | bytes 786436
  82.2 47.5 %reduce-scatter.4.cloned.1.call-start = ((), (), s32[]{:S(2)}) async-start(), calls=%async_computation.3 | async-start | bytes 786432 | tf_op jit(solution)/shard_map/reduce_scatter | solution.py:71
  93.8 101.3 %reduce-scatter.8.cloned.1.call-start = ((), (), s32[]{:S(2)}) async-start(), calls=%async_computation.6 | async-start | bytes 2228224 | tf_op jit(solution)/shard_map/reduce_scatter | solution.py:65
  112.8 2.7 %copy-start = (bf16[2,256,1024]{2,1,0:T(8,128)(2,1)S(1)}, bf16[2,256,1024]{2,1,0:T(8,128)(2,1)}, u32[]{:S(2)}) copy-start(bf16[2,256,1024]{2,1,0:T(8,128)(2,1)} %reduce-scatter.6.cloned.1.call-done) | copy-start | bytes 3145732
Sparse Core Ops, SparseCore 0:
  9.5 53.0 all-gather.1
  82.3 30.4 reduce-scatter.5
  115.0 14.6 reduce-scatter.3
  133.3 61.7 reduce-scatter.7
where the time goes:
time: 209 us
  waiting for transfers between devices  149 us (71%)
  matrix products  37.7 us (18%)
  between operations  13.2 us (6%)
  blocking collectives  5.64 us (3%)
  other arithmetic  2.27 us (1%)
    reduce_scatter x1, waiting for transfers between devices, body(): lax.psum_scatter(jnp.sum(factor[:, :, None] * picked, axis=0).astype(jnp....  65.4 us
    all_gather x1, waiting for transfers between devices, body(): lax.all_gather(tokens, 'expert', axis=0, tiled=True)  53.9 us
    reduce_scatter x1, waiting for transfers between devices, body(): lax.psum_scatter(partial_value.astype(jnp.bfloat16), 'tensor', scatter_di...  18.9 us
    reduce_scatter x1, waiting for transfers between devices, body(): lax.psum_scatter(shared_part, 'tensor', scatter_dimension=1, tiled=True)  10.3 us
    dot_general x1, matrix products, body(): jnp.einsum('lcf,lfd->lcd', hidden, w_down, preferred_element_type=jnp.flo...  9.58 us
    dot_general x1, matrix products, body(): jnp.dot(shared_hidden, shared_down, preferred_element_type=jnp.float32)  7.84 us
    all_gather x1, blocking collectives, body(): return lax.all_gather(mixed, 'tensor', axis=1, tiled=True)  5.64 us
    dot_general x1, matrix products, body(): jnp.einsum('lcd,ldf->lcf', dispatched, w_gate, preferred_element_type=jnp...  5.42 us
  transfers between devices with their start and end apart: 4, of which 4 were waited for; matrix products, arithmetic and copies ran while one was open for 9% of the time, Pallas kernels for 0%

commit v1 on v0

v1 whole, which is shorter than its diff:
```python
import functools
import math

import jax
import jax.numpy as jnp
from jax import lax
from jax.experimental import pallas as pl
from jax.experimental.pallas import tpu as pltpu
from jax.sharding import PartitionSpec as P

MESH = pl.DeviceIdType.MESH


def here(width):
    e = lax.axis_index("expert")
    return lax.div(e, 4), lax.rem(lax.div(e, 2), 2), lax.rem(e, 2), lax.axis_index("tensor")


def expert_at(line, side, core):
    return (line * 2 + side) * 2 + core


def peers_of(t, width):
    return [lax.rem(t + j, width) for j in range(1, width)]


def barrier(z, x, c, t, lines, width):
    sem = pltpu.get_barrier_semaphore()

    def greet(**where):
        pl.semaphore_signal(sem, inc=1, device_id=where, device_id_type=MESH)

    @pl.when(z > 0)
    def _():
        greet(expert=expert_at(z - 1, x, c))

    @pl.when(z < lines - 1)
    def _():
        greet(expert=expert_at(z + 1, x, c))

    greet(expert=expert_at(z, 1 - x, c))
    greet(expert=expert_at(z, x, 1 - c))
    for p in peers_of(t, width):
        greet(tensor=p)

    pl.semaphore_wait(sem, 1 + width + lax.min(z, 1) + lax.min(lines - 1 - z, 1))


def remote(src, dst, send, recv, **where):
    return pltpu.make_async_remote_copy(
        src_ref=src, dst_ref=dst, send_sem=send, recv_sem=recv, device_id=where, device_id_type=MESH
    )


def ring_of(z, k, lines):
    if k == 0:
        return [(z, None)]
    return [(z - k, z - k >= 0), (z + k, z + k < lines)]


def guarded(cond, fn):
    if cond is None:
        fn()
    else:
        pl.when(cond)(fn)


def gather_kernel(lines, width, x_ref, out, own_sem, z_send, z_recv, x_send, x_recv, y_send, y_recv, c_send, c_recv):
    z, x, c, t = here(width)
    barrier(z, x, c, t, lines, width)
    me = expert_at(z, x, c)

    def own(line):
        return out.at[expert_at(line, x, c)]

    def line_copy(src, line, up):
        to = z + 1 if up else z - 1
        d = 1 if up else 0
        return remote(src, own(line), z_send.at[d, line], z_recv.at[d, line], expert=expert_at(to, x, c))

    def side_copy(src, line, side):
        return remote(
            src, out.at[expert_at(line, side, c), t], x_send.at[line], x_recv.at[line],
            expert=expert_at(z, 1 - x, c),
        )

    def wide_copy(line, part, j, slot):
        ref = out.at[expert_at(line, 1 - x, c), part]
        return remote(ref, ref, y_send.at[line, j], y_recv.at[line, slot], tensor=lax.rem(t + j + 1, width))

    def core_copy(src, line, side, core):
        return remote(
            src, out.at[expert_at(line, side, core)], c_send.at[line, side], c_recv.at[line, side],
            expert=expert_at(z, x, 1 - c),
        )

    keep = pltpu.make_async_copy(x_ref, out.at[me], own_sem)
    keep.start()

    def first(line, k):
        def go():
            src = x_ref if k == 0 else own(line)

            def send_up():
                line_copy(src, line, True).start()

            def send_down():
                line_copy(src, line, False).start()

            if k == 0:
                pl.when(z < lines - 1)(send_up)
                pl.when(z > 0)(send_down)
            side_copy(src.at[t], line, x).start()
            core_copy(src, line, x, c).start()

        return go

    def arrive(line, k, from_below):
        def go():
            line_copy(own(line), line, from_below).wait_recv()
            if from_below:
                pl.when(z < lines - 1)(lambda: line_copy(own(line), line, True).start())
            else:
                pl.when(z > 0)(lambda: line_copy(own(line), line, False).start())
            side_copy(own(line).at[t], line, x).start()
            core_copy(own(line), line, x, c).start()

        return go

    for k in range(lines + 2):
        if k < lines:
            for i, (line, ok) in enumerate(ring_of(z, k, lines)):
                guarded(ok, first(line, 0) if k == 0 else arrive(line, k, i == 0))
        if 1 <= k <= lines:
            for line, ok in ring_of(z, k - 1, lines):

                def pass_on(line=line):
                    side_copy(out.at[expert_at(line, 1 - x, c), t], line, 1 - x).wait_recv()
                    for j in range(width - 1):
                        wide_copy(line, t, j, j).start()

                guarded(ok, pass_on)
        if k >= 2:
            for line, ok in ring_of(z, k - 2, lines):

                def to_core(line=line):
                    for j in range(width - 1):
                        part = lax.rem(t + 2 * width - j - 1, width)
                        wide_copy(line, part, j, j).wait_recv()
                    core_copy(out.at[expert_at(line, 1 - x, c)], line, 1 - x, c).start()

                guarded(ok, to_core)

    keep.wait()
    for line in range(lines):
        for side in range(2):
            core_copy(out.at[expert_at(line, side, 1 - c)], line, side, 1 - c).wait()
        side_copy(out.at[expert_at(line, x, c), t], line, x).wait_send()
        for j in range(width - 1):
            wide_copy(line, t, j, j).wait_send()
        pl.when((z < lines - 1) & (line <= z))(lambda line=line: line_copy(own(line), line, True).wait_send())
        pl.when((z > 0) & (line >= z))(lambda line=line: line_copy(own(line), line, False).wait_send())


def gather(tokens, experts, width):
    rows, depth = tokens.shape
    lines = experts // 4
    part = rows // width
    dma = pltpu.SemaphoreType.DMA
    out = pl.pallas_call(
        functools.partial(gather_kernel, lines, width),
        out_shape=jax.ShapeDtypeStruct((experts, width, part, depth), tokens.dtype),
        in_specs=[pl.BlockSpec(memory_space=pltpu.VMEM)],
        out_specs=pl.BlockSpec(memory_space=pltpu.VMEM),
        scratch_shapes=[
            dma,
            dma((2, lines)),
            dma((2, lines)),
            dma((lines,)),
            dma((lines,)),
            dma((lines, max(1, width - 1))),
            dma((lines, max(1, width - 1))),
            dma((lines, 2)),
            dma((lines, 2)),
        ],
        compiler_params=pltpu.CompilerParams(collective_id=0, has_side_effects=True),
    )(tokens.reshape(width, part, depth))
    return out.reshape(experts * rows, depth)


def combine_kernel(
    lines, width, p_ref, s_ref, o_ref, cin, aout, yin, xout, xin, zout, zin, fin,
    c_send, c_recv, y_send, y_recv, x_send, x_recv, z_send, z_recv, f_send, f_recv,
):
    z, x, c, t = here(width)
    f32, half = jnp.float32, jnp.bfloat16
    barrier(z, x, c, t, lines, width)

    def core_copy(line, side):
        return remote(
            p_ref.at[expert_at(line, side, 1 - c)], cin.at[line, side], c_send.at[line, side], c_recv.at[line, side],
            expert=expert_at(z, x, 1 - c),
        )

    def wide_copy(line, j):
        to = lax.rem(t + j + 1, width)
        return remote(aout.at[line, to], yin.at[line, j], y_send.at[line, j], y_recv.at[line, j], tensor=to)

    def side_copy(line):
        return remote(xout.at[line], xin.at[line], x_send.at[line], x_recv.at[line], expert=expert_at(z, 1 - x, c))

    def line_copy(line, up):
        d = 1 if up else 0
        to = z + 1 if up else z - 1
        return remote(zout.at[line], zin.at[d, line], z_send.at[line], z_recv.at[d, line], expert=expert_at(to, x, c))

    def last_copy(j):
        to = lax.rem(t + j + 1, width)
        return remote(fin.at[t], fin.at[t], f_send.at[j], f_recv.at[j], tensor=to)

    order = [ring_of(z, k, lines) for k in range(lines - 1, -1, -1)]
    for level in order:
        for side in (1 - x, x):
            for line, ok in level:
                guarded(ok, lambda line=line, side=side: core_copy(line, side).start())

    def other_side(line):
        core_copy(line, 1 - x).wait_recv()
        aout[line] = (p_ref[expert_at(line, 1 - x, c)].astype(f32) + cin[line, 1 - x].astype(f32)).astype(half)
        for j in range(width - 1):
            wide_copy(line, j).start()

    def cross(line):
        acc = aout[line, t].astype(f32)
        for j in range(width - 1):
            wide_copy(line, j).wait_recv()
            acc = acc + yin[line, j].astype(f32)
        xout[line] = acc.astype(half)
        side_copy(line).start()

    def near(line, dst):
        core_copy(line, x).wait_recv()
        dst[line] = (p_ref[expert_at(line, x, c)].astype(f32) + cin[line, x].astype(f32)).astype(half)
        side_copy(line).wait_recv()
        dst[line, t] = (
            p_ref[expert_at(line, x, c), t].astype(f32) + cin[line, x, t].astype(f32) + xin[line].astype(f32)
        ).astype(half)

    def onward(line, up):
        near(line, zout)

        def add():
            line_copy(line, up).wait_recv()
            zout[line] = (zout[line].astype(f32) + zin[1 if up else 0, line].astype(f32)).astype(half)

        pl.when(z > 0 if up else z < lines - 1)(add)
        line_copy(line, up).start()

    def finish():
        near(z, zout)
        fin[t] = (zout[z].astype(f32) + s_ref[...]).astype(half)
        for up in (False, True):

            def add(up=up):
                line_copy(z, up).wait_recv()
                fin[t] = (fin[t].astype(f32) + zin[1 if up else 0, z].astype(f32)).astype(half)

            pl.when(z > 0 if up else z < lines - 1)(add)
        for j in range(width - 1):
            last_copy(j).start()

    for k in range(lines + 2):
        if k < lines:
            for line, ok in order[k]:
                guarded(ok, functools.partial(other_side, line))
        if 1 <= k <= lines:
            for line, ok in order[k - 1]:
                guarded(ok, functools.partial(cross, line))
        if k >= 2:
            level = order[k - 2]
            if len(level) == 1:
                finish()
            else:
                for i, (line, ok) in enumerate(level):
                    guarded(ok, functools.partial(onward, line, i == 1))

    for j in range(width - 1):
        part = lax.rem(t + 2 * width - j - 1, width)
        remote(fin.at[part], fin.at[part], f_send.at[j], f_recv.at[j], tensor=part).wait_recv()
    acc = fin[0].astype(f32)
    for j in range(1, width):
        acc = acc + fin[j].astype(f32)
    o_ref[...] = acc.astype(half)

    for j in range(width - 1):
        last_copy(j).wait_send()
    for line in range(lines):
        for side in range(2):
            core_copy(line, side).wait_send()
        for j in range(width - 1):
            wide_copy(line, j).wait_send()
        side_copy(line).wait_send()
        pl.when(line != z)(lambda line=line: line_copy(line, True).wait_send())


def combine(partial, shared, experts, width):
    total, depth = partial.shape
    rows = total // experts
    part = rows // width
    lines = experts // 4
    peers = max(1, width - 1)
    dma = pltpu.SemaphoreType.DMA
    half = jnp.bfloat16
    block = (width, part, depth)
    vmem = pl.BlockSpec(memory_space=pltpu.VMEM)
    out = pl.pallas_call(
        functools.partial(combine_kernel, lines, width),
        out_shape=jax.ShapeDtypeStruct(block, half),
        in_specs=[vmem, vmem],
        out_specs=vmem,
        scratch_shapes=[
            pltpu.VMEM((lines, 2) + block, half),
            pltpu.VMEM((lines,) + block, half),
            pltpu.VMEM((lines, peers, part, depth), half),
            pltpu.VMEM((lines, part, depth), half),
            pltpu.VMEM((lines, part, depth), half),
            pltpu.VMEM((lines,) + block, half),
            pltpu.VMEM((2, lines) + block, half),
            pltpu.VMEM((width,) + block, half),
            dma((lines, 2)),
            dma((lines, 2)),
            dma((lines, peers)),
            dma((lines, peers)),
            dma((lines,)),
            dma((lines,)),
            dma((lines,)),
            dma((2, lines)),
            dma((peers,)),
            dma((peers,)),
        ],
        compiler_params=pltpu.CompilerParams(collective_id=1, has_side_effects=True),
    )(partial.reshape((experts,) + block), shared.reshape(block))
    return out.reshape(rows, depth)


def place_rows(expert_ids, gate_probs, expert):
    hits = expert_ids == expert
    row_hit = jnp.sum(hits.astype(jnp.float32), axis=1)
    total_rows = row_hit.shape[0]
    block = math.gcd(total_rows, 128)
    blocks = row_hit.reshape(total_rows // block, block)
    lower = jnp.arange(block, dtype=jnp.int32)
    strict = (lower[:, None] < lower[None, :]).astype(jnp.float32)
    inside = jnp.dot(blocks, strict, precision=lax.Precision.HIGHEST)
    sums = jnp.sum(blocks, axis=1)
    offsets = jnp.cumsum(sums) - sums
    before = (inside + offsets[:, None]).reshape(total_rows)
    target = jnp.where(row_hit > 0.5, before, -1.0).astype(jnp.int32)
    weight = jnp.sum(jnp.where(hits, gate_probs, 0.0), axis=1)
    return (target, weight)


def body(experts, width, tokens, expert_ids, gate_probs, w_gate, w_up, w_down, shared_gate, shared_up, shared_down):
    f32, half = jnp.float32, jnp.bfloat16
    local_count = w_gate.shape[0]
    capacity = 4 * tokens.shape[0]
    first_expert = lax.axis_index("expert") * local_count
    local_experts = first_expert + jnp.arange(local_count, dtype=jnp.int32)
    everyone = gather(tokens, experts, width)
    targets, weights = jax.vmap(lambda expert: place_rows(expert_ids, gate_probs, expert))(local_experts)
    positions = jnp.arange(capacity, dtype=jnp.int32)
    hit = positions[None, :, None] == targets[:, None, :]
    slot_weight = jnp.sum(jnp.where(hit, weights[:, None, :], 0.0), axis=2)
    picker = hit.astype(half)
    dispatched = jnp.einsum("lcr,rd->lcd", picker, everyone, preferred_element_type=f32).astype(half)
    gate = jnp.einsum("lcd,ldf->lcf", dispatched, w_gate, preferred_element_type=f32)
    upper = jnp.einsum("lcd,ldf->lcf", dispatched, w_up, preferred_element_type=f32)
    hidden = (jax.nn.silu(gate) * upper * slot_weight[:, :, None]).astype(half)
    slot_out = jnp.einsum("lcf,lfd->lcd", hidden, w_down, preferred_element_type=f32).astype(half)
    partial = jnp.einsum("lcr,lcd->rd", picker, slot_out, preferred_element_type=f32).astype(half)
    sgate = jnp.dot(tokens, shared_gate, preferred_element_type=f32)
    supper = jnp.dot(tokens, shared_up, preferred_element_type=f32)
    shared_hidden = (jax.nn.silu(sgate) * supper).astype(half)
    shared = jnp.dot(shared_hidden, shared_down, preferred_element_type=f32)
    return combine(partial, shared, experts, width)


def solution(mesh):
    placed = (
        P("expert", None),
        P(),
        P(),
        P("expert", None, "tensor"),
        P("expert", None, "tensor"),
        P("expert", "tensor", None),
        P(None, "tensor"),
        P(None, "tensor"),
        P("tensor", None),
    )
    experts, width = mesh.shape["expert"], mesh.shape["tensor"]
    return jax.shard_map(
        functools.partial(body, experts, width),
        mesh=mesh, in_specs=placed, out_specs=P("expert", None), check_vma=False,
    )
```

time: 209 us -> 112 us (0.54)
  waiting for transfers between devices: 149 us -> 0 us
  Pallas kernels: 0 us -> 77.2 us
  between operations: 13.2 us -> 0.08 us
  matrix products: 37.7 us -> 31.2 us
  blocking collectives: 5.64 us -> 0 us
    reduce_scatter x3 -> x0, waiting for transfers between devices: 94.7 us -> none  [the longest x1 65.4 us: body(): lax.psum_scatter(jnp.sum(factor[:, :, None] * picked, axis=0).astype(jnp....]
    pallas_call x0 -> x2, Pallas kernels: none -> 77.2 us  [the longest x1 39.4 us: combine(): pl.pallas_call(functools.partial(combine_kernel, lines, width), out_shape...]
    all_gather x1 -> x0, waiting for transfers between devices: 53.9 us -> none  [body(): lax.all_gather(tokens, 'expert', axis=0, tiled=True)]
    dot_general x7 -> x6, matrix products: 37.6 us -> 31.1 us  [the longest x1 8.63 us: body(): jnp.einsum('lcr,lcd->rd', picker, slot_out, preferred_element_type=f32)]
    all_gather x1 -> x0, blocking collectives: 5.64 us -> none  [body(): return lax.all_gather(mixed, 'tensor', axis=1, tiled=True)]
  transfers between devices with their start and end apart: 4 -> 0, of which waited for: 4 -> 0; matrix products, arithmetic and copies ran while one was open for 9% -> 0% of each run, Pallas kernels for 0% -> 0%
where the time goes in v1:
time: 112 us
  Pallas kernels  77.2 us (69%)
  matrix products  31.2 us (28%)
  other arithmetic  1.96 us (2%)
  local copies, waits for them, and re-layouts  1.68 us (2%)
    pallas_call x1, Pallas kernels, combine(): pl.pallas_call(functools.partial(combine_kernel, lines, width), out_shape...  39.4 us
    pallas_call x1, Pallas kernels, gather(): pl.pallas_call(functools.partial(gather_kernel, lines, width), out_shape=...  37.8 us
    dot_general x1, matrix products, body(): jnp.einsum('lcr,lcd->rd', picker, slot_out, preferred_element_type=f32)  8.63 us
    dot_general x1, matrix products, body(): shared = jnp.dot(shared_hidden, shared_down, preferred_element_type=f32)  7.22 us
    dot_general x1, matrix products, body(): jnp.einsum('lcr,rd->lcd', picker, everyone, preferred_element_type=f32)  4.96 us
    dot_general x1, matrix products, body(): jnp.einsum('lcd,ldf->lcf', dispatched, w_gate, preferred_element_type=f32)  4.65 us
    dot_general x1, matrix products, body(): sgate = jnp.dot(tokens, shared_gate, preferred_element_type=f32)  3.7 us

profile of v1, /device:TPU:0, one launch (start us, length us, event | category | flops | bytes accessed | tf_op | source)
XLA Modules:
  0.0 112.1 jit_solution(10354561014845696969)
XLA Ops:
  0.0 0.9 fusion.16
  0.9 0.1 bitcast_reduce_fusion
  1.0 0.2 reduce_window_sum.11
  1.2 0.1 fusion.3
  1.3 0.1 fusion.17
  1.4 37.8 %shard_map.91 = bf16[16,2,32,2048]{3,2,1,0:T(8,128)(2,1)} custom-call(bf16[2,32,2048]{2,1,0:T(8,128)(2,1)} %bitcast.35), custom_call_target="tpu_custom_call" | custom-call | tf_op jit(solution)/shard_map/pallas_call | solution.py:170
  39.1 5.0 %convolution_convert_fusion = bf16[2,256,2048]{2,1,0:T(8,128)(2,1)S(1)} fusion(bf16[1024,2048,1]{1,0,2:T(8,128)(2,1)} %bitcast.34, s32[2,1024]{1,0:T(2,128)S(1)} %fusion.17), kind=kOutput, calls=%fused_computation.1 | convolution fusion | flops 2149056512 | bytes 6299648 | tf_op jit(solution)/shard_map/lcr,rd->lcd/dot_general | solution.py:375
  44.1 0.0 copy-start.1
  44.1 4.7 %fusion.21 = f32[2,256,704]{1,2,0:T(8,128)S(1)} fusion(bf16[2,256,2048]{2,1,0:T(8,128)(2,1)S(1)} %convolution_convert_fusion, bf16[2,2048,704]{1,2,0:T(8,128)(2,1)} %param.12), kind=kOutput, calls=%fused_computation.34 | convolution fusion | flops 1476395008 | bytes 9306112 | tf_op jit(solution)/shard_map/lcd,ldf->lcf/dot_general | solution.py:376
  48.8 0.7 select_reduce_fusion
  49.5 0.0 copy-done.1
  49.5 1.9 %fusion.2 = bf16[2,256,704]{1,2,0:T(8,128)(2,1)S(1)} fusion(bf16[2,256,2048]{2,1,0:T(8,128)(2,1)S(1)} %convolution_convert_fusion, bf16[2,2048,704]{1,2,0:T(8,128)(2,1)S(1)} %copy-done.1, f32[2,256,704]{1,2,0:T(8,128)S(1)} %fusion.21, f32[2,256]{1,0:T(2,128)S(1)} %select_reduce_fusion), kind=kOutput, calls=%fused_computation.9 | convolution fusion | flops 1478918144 | bytes 10029056 | tf_op jit(solution)/shard_map/lcd,ldf->lcf/dot_general | solution.py:377
  51.4 0.0 copy-start
  51.4 8.6 %bitcast_convert_fusion = bf16[1024,2048]{1,0:T(8,128)(2,1)} fusion(s32[2,1024]{1,0:T(2,128)S(1)} %fusion.17, bf16[2,256,704]{1,2,0:T(8,128)(2,1)S(1)} %fusion.2, bf16[2,704,2048]{2,1,0:T(8,128)(2,1)} %param.14), kind=kOutput, calls=%fused_computation | convolution fusion | flops 3627548672 | bytes 10690560 | tf_op jit(solution)/shard_map/lcr,lcd->rd/dot_general | solution.py:380
  60.1 0.0 copy-done
  60.1 3.7 %fusion.22 = f32[64,1408]{1,0:T(8,128)S(1)} fusion(bf16[64,2048]{1,0:T(8,128)(2,1)S(1)} %copy-done, bf16[2048,1408]{1,0:T(8,128)(2,1)} %param.15), kind=kOutput, calls=%fused_computation.35 | convolution fusion | flops 369098752 | bytes 6389760 | tf_op jit(solution)/shard_map/dot_general | solution.py:381
  63.8 7.2 %fusion.4 = f32[64,2048]{1,0:T(8,128)} fusion(bf16[1408,2048]{1,0:T(8,128)(2,1)} %param.17, bf16[64,2048]{1,0:T(8,128)(2,1)S(1)} %copy-done, bf16[2048,1408]{1,0:T(8,128)(2,1)} %param.16, f32[64,1408]{1,0:T(8,128)S(1)} %fusion.22), kind=kOutput, calls=%fused_computation.12 | convolution fusion | flops 738738176 | bytes 12681216 | tf_op jit(solution)/shard_map/dot_general | solution.py:384
  71.0 39.4 %shard_map.92 = bf16[2,32,2048]{2,1,0:T(8,128)(2,1)} custom-call(bf16[16,2,32,2048]{3,2,1,0:T(8,128)(2,1)} %bitcast.33, f32[2,32,2048]{2,1,0:T(8,128)} %bitcast.36), custom_call_target="tpu_custom_call" | custom-call | tf_op jit(solution)/shard_map/pallas_call | solution.py:316
  110.4 1.7 %copy.24 = bf16[64,2048]{1,0:T(8,128)(2,1)} copy(bf16[64,2048]{1,0:T(8,128)(2,1)} %bitcast.37) | data formatting | bytes 524288
  (2 shorter events, 0.0 us)
Async XLA Ops:
  44.1 5.4 %copy-start.1 = (bf16[2,2048,704]{1,2,0:T(8,128)(2,1)S(1)}, bf16[2,2048,704]{1,2,0:T(8,128)(2,1)}, u32[]{:S(2)}) copy-start(bf16[2,2048,704]{1,2,0:T(8,128)(2,1)} %param.13) | copy-start | bytes 17301508
  51.4 8.6 %copy-start = (bf16[64,2048]{1,0:T(8,128)(2,1)S(1)}, bf16[64,2048]{1,0:T(8,128)(2,1)}, u32[]{:S(2)}) copy-start(bf16[64,2048]{1,0:T(8,128)(2,1)} %param.9) | copy-start | bytes 786436

commit v2 on v1

--- a/solution.py
+++ b/solution.py
@@ -65,10 +65,30 @@
         pl.when(cond)(fn)
 
 
-def gather_kernel(lines, width, x_ref, out, own_sem, z_send, z_recv, x_send, x_recv, y_send, y_recv, c_send, c_recv):
+def gather_kernel(lines, width, x_ref, flat_ref, sg_hbm, su_hbm, sd_hbm, out, s_ref, sg, su, sd, w_sem, own_sem, z_send, z_recv, x_send, x_recv, y_send, y_recv, c_send, c_recv):
     z, x, c, t = here(width)
+    loads = [
+        pltpu.make_async_copy(src, dst, w_sem.at[i])
+        for i, (src, dst) in enumerate(((sg_hbm, sg), (su_hbm, su), (sd_hbm, sd)))
+    ]
+    for load in loads:
+        load.start()
     barrier(z, x, c, t, lines, width)
     me = expert_at(z, x, c)
+    hidden = sg.shape[1]
+    cuts = [(i, min(256, hidden - i)) for i in range(0, hidden, 256)]
+
+    def shared_piece(i):
+        at, size = cuts[i]
+        f32 = jnp.float32
+        g = jnp.dot(flat_ref[...], sg[:, at : at + size], preferred_element_type=f32)
+        u = jnp.dot(flat_ref[...], su[:, at : at + size], preferred_element_type=f32)
+        h = (g / (1.0 + jnp.exp(-g)) * u).astype(jnp.bfloat16)
+        depth = s_ref.shape[1]
+        step = math.gcd(depth, 512)
+        for n in range(0, depth, step):
+            piece = jnp.dot(h, sd[at : at + size, n : n + step], preferred_element_type=f32)
+            s_ref[:, n : n + step] = piece if i == 0 else s_ref[:, n : n + step] + piece
 
     def own(line):
         return out.at[expert_at(line, x, c)]
@@ -150,6 +170,12 @@
                     core_copy(out.at[expert_at(line, 1 - x, c)], line, 1 - x, c).start()
 
                 guarded(ok, to_core)
+        if k == 1:
+            for load in loads:
+                load.wait()
+        for i in range(len(cuts)):
+            if k == 1 + i * max(1, lines - 1) // len(cuts):
+                shared_piece(i)
 
     keep.wait()
     for line in range(lines):
@@ -162,17 +188,25 @@
         pl.when((z > 0) & (line >= z))(lambda line=line: line_copy(own(line), line, False).wait_send())
 
 
-def gather(tokens, experts, width):
+def gather(tokens, shared_gate, shared_up, shared_down, experts, width):
     rows, depth = tokens.shape
     lines = experts // 4
     part = rows // width
     dma = pltpu.SemaphoreType.DMA
-    out = pl.pallas_call(
+    vmem, hbm = pl.BlockSpec(memory_space=pltpu.VMEM), pl.BlockSpec(memory_space=pltpu.HBM)
+    out, shared = pl.pallas_call(
         functools.partial(gather_kernel, lines, width),
-        out_shape=jax.ShapeDtypeStruct((experts, width, part, depth), tokens.dtype),
-        in_specs=[pl.BlockSpec(memory_space=pltpu.VMEM)],
-        out_specs=pl.BlockSpec(memory_space=pltpu.VMEM),
+        out_shape=(
+            jax.ShapeDtypeStruct((experts, width, part, depth), tokens.dtype),
+            jax.ShapeDtypeStruct((rows, depth), jnp.float32),
+        ),
+        in_specs=[vmem, vmem, hbm, hbm, hbm],
+        out_specs=(vmem, vmem),
         scratch_shapes=[
+            pltpu.VMEM(shared_gate.shape, shared_gate.dtype),
+            pltpu.VMEM(shared_up.shape, shared_up.dtype),
+            pltpu.VMEM(shared_down.shape, shared_down.dtype),
+            dma((3,)),
             dma,
             dma((2, lines)),
             dma((2, lines)),
@@ -184,12 +218,12 @@
             dma((lines, 2)),
         ],
         compiler_params=pltpu.CompilerParams(collective_id=0, has_side_effects=True),
-    )(tokens.reshape(width, part, depth))
-    return out.reshape(experts * rows, depth)
+    )(tokens.reshape(width, part, depth), tokens, shared_gate, shared_up, shared_down)
+    return out.reshape(experts * rows, depth), shared
 
 
 def combine_kernel(
-    lines, width, p_ref, s_ref, o_ref, cin, aout, yin, xout, xin, zout, zin, fin,
+    lines, width, sel_ref, slot_ref, s_ref, o_ref, p_ref, cin, aout, yin, xout, xin, zout, zin, fin,
     c_send, c_recv, y_send, y_recv, x_send, x_recv, z_send, z_recv, f_send, f_recv,
 ):
     z, x, c, t = here(width)
@@ -219,10 +253,17 @@
         return remote(fin.at[t], fin.at[t], f_send.at[j], f_recv.at[j], tensor=to)
 
     order = [ring_of(z, k, lines) for k in range(lines - 1, -1, -1)]
-    for level in order:
-        for side in (1 - x, x):
-            for line, ok in level:
-                guarded(ok, lambda line=line, side=side: core_copy(line, side).start())
+
+    def produce(line, side):
+        row = line * 2 + side
+        depth = slot_ref.shape[1]
+        step = math.gcd(depth, 512)
+        block = p_ref.shape[1:3]
+        for n in range(0, depth, step):
+            piece = jnp.dot(sel_ref[row], slot_ref[:, n : n + step], preferred_element_type=f32)
+            piece = piece.reshape((2,) + block + (step,)).astype(half)
+            p_ref[pl.ds(row * 2, 2), :, :, n : n + step] = piece
+        core_copy(line, side).start()
 
     def other_side(line):
         core_copy(line, 1 - x).wait_recv()
@@ -269,15 +310,19 @@
         for j in range(width - 1):
             last_copy(j).start()
 
-    for k in range(lines + 2):
+    for k in range(lines + 3):
         if k < lines:
-            for line, ok in order[k]:
-                guarded(ok, functools.partial(other_side, line))
+            for side in (1 - x, x):
+                for line, ok in order[k]:
+                    guarded(ok, functools.partial(produce, line, side))
         if 1 <= k <= lines:
             for line, ok in order[k - 1]:
+                guarded(ok, functools.partial(other_side, line))
+        if 2 <= k <= lines + 1:
+            for line, ok in order[k - 2]:
                 guarded(ok, functools.partial(cross, line))
-        if k >= 2:
-            level = order[k - 2]
+        if k >= 3:
+            level = order[k - 3]
             if len(level) == 1:
                 finish()
             else:
@@ -303,8 +348,8 @@
         pl.when(line != z)(lambda line=line: line_copy(line, True).wait_send())
 
 
-def combine(partial, shared, experts, width):
-    total, depth = partial.shape
+def combine(chosen, slot_out, shared, experts, width):
+    total, depth = chosen.shape[0], slot_out.shape[1]
     rows = total // experts
     part = rows // width
     lines = experts // 4
@@ -316,9 +361,10 @@
     out = pl.pallas_call(
         functools.partial(combine_kernel, lines, width),
         out_shape=jax.ShapeDtypeStruct(block, half),
-        in_specs=[vmem, vmem],
+        in_specs=[vmem, vmem, vmem],
         out_specs=vmem,
         scratch_shapes=[
+            pltpu.VMEM((experts,) + block, half),
             pltpu.VMEM((lines, 2) + block, half),
             pltpu.VMEM((lines,) + block, half),
             pltpu.VMEM((lines, peers, part, depth), half),
@@ -339,7 +385,7 @@
             dma((peers,)),
         ],
         compiler_params=pltpu.CompilerParams(collective_id=1, has_side_effects=True),
-    )(partial.reshape((experts,) + block), shared.reshape(block))
+    )(chosen.reshape(experts // 2, 2 * rows, -1), slot_out, shared.reshape(block))
     return out.reshape(rows, depth)
 
 
@@ -366,7 +412,7 @@
     capacity = 4 * tokens.shape[0]
     first_expert = lax.axis_index("expert") * local_count
     local_experts = first_expert + jnp.arange(local_count, dtype=jnp.int32)
-    everyone = gather(tokens, experts, width)
+    everyone, shared = gather(tokens, shared_gate, shared_up, shared_down, experts, width)
     targets, weights = jax.vmap(lambda expert: place_rows(expert_ids, gate_probs, expert))(local_experts)
     positions = jnp.arange(capacity, dtype=jnp.int32)
     hit = positions[None, :, None] == targets[:, None, :]
@@ -377,12 +423,13 @@
     upper = jnp.einsum("lcd,ldf->lcf", dispatched, w_up, preferred_element_type=f32)
     hidden = (jax.nn.silu(gate) * upper * slot_weight[:, :, None]).astype(half)
     slot_out = jnp.einsum("lcf,lfd->lcd", hidden, w_down, preferred_element_type=f32).astype(half)
-    partial = jnp.einsum("lcr,lcd->rd", picker, slot_out, preferred_element_type=f32).astype(half)
-    sgate = jnp.dot(tokens, shared_gate, preferred_element_type=f32)
-    supper = jnp.dot(tokens, shared_up, preferred_element_type=f32)
-    shared_hidden = (jax.nn.silu(sgate) * supper).astype(half)
-    shared = jnp.dot(shared_hidden, shared_down, preferred_element_type=f32)
-    return combine(partial, shared, experts, width)
+    columns = jnp.arange(local_count * capacity, dtype=jnp.int32)
+    chosen = False
+    for i in range(local_count):
+        place = jnp.where(targets[i] >= 0, targets[i] + i * capacity, -1)
+        chosen = chosen | (place[:, None] == columns[None, :])
+    chosen = chosen.astype(half)
+    return combine(chosen, slot_out.reshape(local_count * capacity, -1), shared, experts, width)
 
 
 def solution(mesh):

time: 112 us -> 101 us (0.902)
  matrix products: 31.2 us -> 17.2 us
  Pallas kernels: 77.2 us -> 78.9 us
    dot_general x4 -> x1, matrix products: 21.5 us -> 9.62 us  [body(): jnp.einsum('lcf,lfd->lcd', hidden, w_down, preferred_element_type=f32)]
    dot_general x1, matrix products: 4.65 us -> 2.79 us  [body(): jnp.einsum('lcd,ldf->lcf', dispatched, w_gate, preferred_element_type=f32)]
    pallas_call x1, Pallas kernels: 39.4 us -> 40.8 us  [combine(): pl.pallas_call(functools.partial(combine_kernel, lines, width), out_shape...]
    convert_element_type x0 -> x1, other arithmetic: none -> 1.26 us  [body(): chosen = chosen.astype(half)]
where the time goes in v2:
time: 101 us
  Pallas kernels  78.9 us (78%)
  matrix products  17.2 us (17%)
  other arithmetic  2.81 us (3%)
  local copies, waits for them, and re-layouts  1.68 us (2%)
    pallas_call x1, Pallas kernels, combine(): pl.pallas_call(functools.partial(combine_kernel, lines, width), out_shape...  40.8 us
    pallas_call x1, Pallas kernels, gather(): pl.pallas_call(functools.partial(gather_kernel, lines, width), out_shape=...  38.1 us
    dot_general x1, matrix products, body(): jnp.einsum('lcf,lfd->lcd', hidden, w_down, preferred_element_type=f32)  9.62 us
    dot_general x1, matrix products, body(): jnp.einsum('lcr,rd->lcd', picker, everyone, preferred_element_type=f32)  4.67 us
    dot_general x1, matrix products, body(): jnp.einsum('lcd,ldf->lcf', dispatched, w_gate, preferred_element_type=f32)  2.79 us

profile of v2, /device:TPU:0, one launch (start us, length us, event | category | flops | bytes accessed | tf_op | source)
XLA Modules:
  0.0 100.7 jit_solution(4468209057965447862)
XLA Ops:
  0.0 0.9 fusion.9
  0.9 0.1 bitcast_reduce_fusion
  1.0 0.2 reduce_window_sum.11
  1.2 0.1 fusion.4
  1.3 0.1 fusion.10
  1.4 38.1 %shard_map.91 = (bf16[16,2,32,2048]{3,2,1,0:T(8,128)(2,1)}, f32[64,2048]{1,0:T(8,128)}) custom-call(bf16[2,32,2048]{2,1,0:T(8,128)(2,1)} %bitcast.28, bf16[64,2048]{1,0:T(8,128)(2,1)} %flat_ref.1, bf16[2048,1408]{1,0:T(8,128)(2,1)} %sg_hbm.1, bf16[2048,1408]{1,0:T(8,128)(2,1)} %su_hbm.1, bf16[1408,2048]{1,0:T(8,128)(2,1)} %sd_hbm.1), custom_call_target="tpu_custom_call" | custom-call | tf_op jit(solution)/shard_map/pallas_call | solution.py:197
  39.5 0.0 copy-start
  39.5 4.7 %convolution_convert_fusion = bf16[2,256,2048]{2,1,0:T(8,128)(2,1)S(1)} fusion(bf16[1024,2048,1]{1,0,2:T(8,128)(2,1)} %bitcast.35, s32[2,1024]{1,0:T(2,128)S(1)} %fusion.10), kind=kOutput, calls=%fused_computation | convolution fusion | flops 2149056512 | bytes 6299648 | tf_op jit(solution)/shard_map/lcr,rd->lcd/dot_general | solution.py:421
  44.2 0.0 copy-done
  44.2 2.8 %fusion.15 = f32[2,256,704]{1,2,0:T(8,128)} fusion(bf16[2,256,2048]{2,1,0:T(8,128)(2,1)S(1)} %convolution_convert_fusion, bf16[2,2048,704]{1,2,0:T(8,128)(2,1)S(1)} %copy-done), kind=kOutput, calls=%fused_computation.30 | convolution fusion | flops 1476395008 | bytes 9306112 | tf_op jit(solution)/shard_map/lcd,ldf->lcf/dot_general | solution.py:422
  47.0 0.3 select_reduce_fusion
  47.2 9.6 %convolution_convert_fusion.1 = bf16[2,256,2048]{2,1,0:T(8,128)(2,1)} fusion(bf16[2,704,2048]{2,1,0:T(8,128)(2,1)} %param.14, bf16[2,256,2048]{2,1,0:T(8,128)(2,1)S(1)} %convolution_convert_fusion, bf16[2,2048,704]{1,2,0:T(8,128)(2,1)} %param.13, f32[2,256,704]{1,2,0:T(8,128)} %fusion.15, f32[2,256]{1,0:T(2,128)S(1)} %select_reduce_fusion), kind=kOutput, calls=%fused_computation.1 | convolution fusion | flops 2956361728 | bytes 17172480 | tf_op jit(solution)/shard_map/lcf,lfd->lcd/dot_general | solution.py:425
  56.9 1.3 %fusion.1.sel_ref = bf16[8,128,512]{2,1,0:T(8,128)(2,1)} fusion(s32[8,128]{1,0:T(8,128)S(1)} %bitcast.33, s32[8,128]{1,0:T(8,128)S(1)} %compare_select_fusion.3), kind=kLoop, calls=%fused_computation.7 | loop fusion | flops 2097152 | bytes 1056768 | tf_op jit(solution)/shard_map/convert_element_type | solution.py:431
  58.1 40.8 %shard_map.92 = bf16[2,32,2048]{2,1,0:T(8,128)(2,1)} custom-call(bf16[8,128,512]{2,1,0:T(8,128)(2,1)} %fusion.1.sel_ref, bf16[512,2048]{1,0:T(8,128)(2,1)} %bitcast.27, f32[2,32,2048]{2,1,0:T(8,128)} %bitcast.30), custom_call_target="tpu_custom_call" | custom-call | tf_op jit(solution)/shard_map/pallas_call | solution.py:361
  99.0 1.7 %copy.21 = bf16[64,2048]{1,0:T(8,128)(2,1)} copy(bf16[64,2048]{1,0:T(8,128)(2,1)} %bitcast.29) | data formatting | bytes 524288
  (4 shorter events, 0.0 us)
Async XLA Ops:
  39.5 4.7 %copy-start = (bf16[2,2048,704]{1,2,0:T(8,128)(2,1)S(1)}, bf16[2,2048,704]{1,2,0:T(8,128)(2,1)}, u32[]{:S(2)}) copy-start(bf16[2,2048,704]{1,2,0:T(8,128)(2,1)} %param.12) | copy-start | bytes 17301508
